TPU v7x, 32 devices: a whole 2x2x4 slice. The times are simulated.
32 devices in a mesh: batch: 16 (over z, y, core), rep: 2 (over x).
Axes of the slice: x: 2, y: 2, z: 4, core: 2. Of those that a mesh axis runs over, the one named last changes fastest.
Arguments:
- queries: bfloat16 [2048, 512], P('batch', 'rep'), may hold values from -8 to 8
- passages: bfloat16 [2048, 512], P('batch', 'rep'), may hold values from -8 to 8
- positives: int32 [2048], replicated, may hold values from 0 to 2047, each once
Outputs:
- grad_queries: float32 [2048, 512], P('batch', 'rep')
- grad_passages: float32 [2048, 512], P('batch', 'rep')
Inputs may be any that keep to these rules, and one draw needn't show every extreme that they name: `positives`: each passage is the positive of exactly one query.
All inputs are finite; a program needn't handle non-finite values.
Results may differ from a plain program's by a relative error of at most 0.0013.
Values may be sent and summed in bfloat16 or wider, within the bound.
A program may use at most 128 MiB of HBM per device.

v0:
```python
import math

import jax
import jax.numpy as jnp
from jax import lax
from jax.sharding import PartitionSpec as P

NEGATIVE = -1e30


def joined(x, axis, combine):
    everything = jax.tree.map(lambda part: lax.all_gather(part, axis), x)
    first = jax.tree.map(lambda part: part[0], everything)

    def turn(k, so_far):
        return combine(so_far, jax.tree.map(lambda part: part[k], everything))

    return lax.fori_loop(1, lax.axis_size(axis), turn, first)


def sweep_blocks(update, running, members, offset):
    piece_rows = members[0].shape[0]
    if piece_rows > 1024 and piece_rows % 512 == 0:

        def advance(carried, block_index):
            sliced = tuple(
                (lax.dynamic_slice_in_dim(member, block_index * 512, 512, 0) for member in members)
            )
            return (update(carried, sliced, offset + block_index * 512), None)

        running, unused = lax.scan(advance, running, jnp.arange(piece_rows // 512, dtype=jnp.int32))
        return running
    return update(running, members, offset)


def combine_pairs(former, latter):
    results = []
    for position in range(0, len(former), 2):
        highest = jnp.maximum(former[position], latter[position])
        summed = former[position + 1] * jnp.exp(former[position] - highest) + latter[
            position + 1
        ] * jnp.exp(latter[position] - highest)
        results.extend([highest, summed])
    return tuple(results)


def pair_scores(local_set, remote_set, logit_scale):
    products = lax.dot_general(
        local_set, remote_set, (((1,), (1,)), ((), ())), preferred_element_type=jnp.float32
    )
    return products * logit_scale


def weighted_sum(
    local_set, local_norm, local_keys, remote_set, remote_norm, remote_keys, logit_scale
):
    scores = pair_scores(local_set, remote_set, logit_scale)
    matches = (local_keys[:, None] == remote_keys[None, :]).astype(jnp.float32)
    weights = (
        jnp.exp(scores - local_norm[:, None])
        + jnp.exp(scores - remote_norm[None, :])
        - 2.0 * matches
    )
    return jnp.dot(weights.astype(jnp.bfloat16), remote_set, preferred_element_type=jnp.float32)


def local(queries, passages, positives):
    own_rows = queries.shape[0]
    half_rows = own_rows // 2
    model_width = queries.shape[1] * lax.axis_size("rep")
    batch_count = lax.axis_size("batch")
    all_rows = batch_count * own_rows
    column_count = batch_count * half_rows
    logit_scale = 1.0 / math.sqrt(model_width)
    batch_index = lax.axis_index("batch")
    rep_index = lax.axis_index("rep")
    block_start = batch_index * own_rows
    half_start = rep_index * half_rows
    query_full, passage_full = (
        lax.all_gather(queries, "rep", axis=1, tiled=True),
        lax.all_gather(passages, "rep", axis=1, tiled=True),
    )
    passage_half = lax.dynamic_slice_in_dim(passage_full, half_start, half_rows, 0)

    def score_update(running, sliced, offset):
        row_high, row_total, column_high, column_total = running
        scores = pair_scores(query_full, sliced[0], logit_scale)
        new_high = jnp.maximum(row_high, jnp.max(scores, axis=1))
        row_total = row_total * jnp.exp(row_high - new_high) + jnp.sum(
            jnp.exp(scores - new_high[:, None]), axis=1
        )
        piece_high = jnp.max(scores, axis=0)
        piece_total = jnp.sum(jnp.exp(scores - piece_high[None, :]), axis=0)
        column_high = lax.dynamic_update_slice_in_dim(column_high, piece_high, offset, 0)
        column_total = lax.dynamic_update_slice_in_dim(column_total, piece_total, offset, 0)
        return (new_high, row_total, column_high, column_total)

    starting = (
        jnp.full((own_rows,), NEGATIVE, jnp.float32),
        jnp.zeros((own_rows,), jnp.float32),
        jnp.full((column_count,), NEGATIVE, jnp.float32),
        jnp.zeros((column_count,), jnp.float32),
    )
    row_high, row_total, column_high, column_total = sweep_blocks(
        score_update,
        starting,
        (lax.all_gather(passage_half, "batch", axis=0, tiled=True),),
        jnp.int32(0),
    )
    row_high, row_total = joined((row_high, row_total), "rep", combine_pairs)
    column_high, column_total = joined((column_high, column_total), "batch", combine_pairs)
    row_norms = lax.all_gather(row_high + jnp.log(row_total), "batch", axis=0, tiled=True)
    column_halves = lax.all_gather(column_high + jnp.log(column_total), "rep", axis=0, tiled=True)
    column_norms = (
        column_halves.reshape(2, batch_count, half_rows).transpose(1, 0, 2).reshape(all_rows)
    )
    row_own = lax.dynamic_slice_in_dim(row_norms, block_start, own_rows, 0)
    column_own = lax.dynamic_slice_in_dim(column_norms, block_start, own_rows, 0)
    positive_own = lax.dynamic_slice_in_dim(positives, block_start, own_rows, 0)
    own_ids = block_start + jnp.arange(own_rows, dtype=jnp.int32)
    all_ids = jnp.arange(all_rows, dtype=jnp.int32)
    cleared = jnp.zeros((own_rows, model_width), jnp.float32)

    def half_order(vector):
        return lax.dynamic_slice_in_dim(
            vector.reshape(batch_count, own_rows), half_start, half_rows, 1
        ).reshape(column_count)

    column_order = half_order(column_norms)
    row_order = half_order(row_norms)
    positive_order = half_order(positives)
    passage_order = half_order(all_ids)
    query_half = lax.dynamic_slice_in_dim(query_full, half_start, half_rows, 0)

    def both_update(running, sliced, offset):
        query_sum, passage_sum = running
        passage_piece, query_piece = sliced
        piece_rows = passage_piece.shape[0]

        def window(vector):
            return lax.dynamic_slice_in_dim(vector, offset, piece_rows, 0)

        query_sum = query_sum + weighted_sum(
            query_full,
            row_own,
            positive_own,
            passage_piece,
            window(column_order),
            window(passage_order),
            logit_scale,
        )
        passage_sum = passage_sum + weighted_sum(
            passage_full,
            column_own,
            own_ids,
            query_piece,
            window(row_order),
            window(positive_order),
            logit_scale,
        )
        return (query_sum, passage_sum)

    query_sum, passage_sum = sweep_blocks(
        both_update,
        (cleared, cleared),
        (
            lax.all_gather(passage_half, "batch", axis=0, tiled=True),
            lax.all_gather(query_half, "batch", axis=0, tiled=True),
        ),
        jnp.int32(0),
    )
    grad_queries, grad_passages = (
        lax.psum_scatter(query_sum * logit_scale, "rep", scatter_dimension=1, tiled=True),
        lax.psum_scatter(passage_sum * logit_scale, "rep", scatter_dimension=1, tiled=True),
    )
    return (grad_queries, grad_passages)


def solution(mesh):
    in_specs = (P("batch", "rep"), P("batch", "rep"), P())
    out_specs = (P("batch", "rep"), P("batch", "rep"))
    return jax.shard_map(local, mesh=mesh, in_specs=in_specs, out_specs=out_specs, check_vma=False)
```

profile of v0, /device:TPU:0, one launch (start us, length us, event | category | flops | bytes accessed | tf_op | source)
XLA Modules:
  0.0 157.9 jit_solution(14381509160952971946)
XLA Ops:
  7.2 0.0 all-gather.9.cloned.1.call-start
  7.2 6.1 %all_gather.39 = bf16[128,512]{1,0:T(8,128)(2,1)S(1)} all-gather(bf16[128,256]{1,0:T(8,128)(2,1)} %param.6), channel_id=1, replica_groups=mesh['batch'=16,'rep'=2] {'rep'}, dimensions={1}, use_global_device_ids=true | all-gather | bytes 196608 | tf_op jit(solution)/shard_map/all_gather | solution.py:81
  13.4 0.6 constant_dynamic-slice_fusion.5
  14.0 0.0 copy-start.1
  14.0 0.0 all-gather.9.cloned.1.call-update
  14.0 0.0 all-gather.11.cloned.1.call-start
  14.1 0.8 copy-done.1
  14.8 4.9 %all_gather.41 = bf16[128,512]{1,0:T(8,128)(2,1)S(1)} all-gather(bf16[128,256]{1,0:T(8,128)(2,1)S(1)} %copy-done.1), channel_id=1, replica_groups=mesh['batch'=16,'rep'=2] {'rep'}, dimensions={1}, use_global_device_ids=true | all-gather | bytes 196608 | tf_op jit(solution)/shard_map/all_gather | solution.py:80
  19.8 0.6 constant_dynamic-slice_fusion.2
  20.4 0.0 all-gather.11.cloned.1.call-update
  20.4 0.0 reduce-scatter.3.cloned.1.call-start
  20.5 0.0 copy-start.2
  20.5 0.1 eq.31
  20.6 0.6 copy-done.2
  21.2 0.1 dynamic_slice.60
  21.3 32.5 %all-gather.9.cloned.1.call-done = bf16[1024,512]{1,0:T(8,128)(2,1)} async-done(((bf16[64,512]{1,0:T(8,128)(2,1)}), bf16[1024,512]{1,0:T(8,128)(2,1)}) %all-gather.9.cloned.1.call-update) | async-done | bytes 1048592 | tf_op jit(solution)/shard_map/all_gather | solution.py:167
  53.8 1.7 %fusion.27 = (f32[128]{0:T(128)S(1)}, f32[1024]{0:T(1024)S(1)}, f32[1024,128]{1,0:T(8,128)S(1)}) fusion(bf16[1024,512]{1,0:T(8,128)(2,1)} %all-gather.9.cloned.1.call-done, bf16[128,512]{1,0:T(8,128)(2,1)S(1)} %all_gather.41), kind=kOutput, calls=%fused_computation.54 | convolution fusion | flops 134609792 | bytes 1708544 | tf_op jit(solution)/shard_map/dot_general | solution.py:48
  55.5 0.0 copy-start
  55.5 19.7 %all-gather.1 = f32[16384]{0:T(1024)S(1)} all-gather(f32[1024]{0:T(1024)S(1)} %get-tuple-element.158), channel_id=3, replica_groups=mesh['batch'=16,'rep'=2] {'batch'}, dimensions={0}, use_global_device_ids=true | all-gather | bytes 69632 | tf_op jit(solution)/shard_map/all_gather | solution.py:12
  75.2 0.4 exponential_reduce_fusion.1
  75.6 17.7 %all-gather.2 = f32[16384]{0:T(1024)S(1)} all-gather(f32[1024]{0:T(1024)S(1)} %get-tuple-element.156), channel_id=4, replica_groups=mesh['batch'=16,'rep'=2] {'batch'}, dimensions={0}, use_global_device_ids=true | all-gather | bytes 69632 | tf_op jit(solution)/shard_map/all_gather | solution.py:12
  93.3 0.9 while.11
  94.2 4.4 %all_gather.49 = f32[2048]{0:T(1024)S(1)} all-gather(f32[1024]{0:T(1024)S(1)} %log_add_fusion), channel_id=1, replica_groups=mesh['batch'=16,'rep'=2] {'rep'}, dimensions={0}, use_global_device_ids=true | all-gather | bytes 12288 | tf_op jit(solution)/shard_map/all_gather | solution.py:113
  98.6 0.1 reshape.67
  98.7 0.1 reshape_reshape.3
  98.7 0.1 constant_dynamic-slice_fusion.4
  98.8 0.1 sub.111
  98.9 4.2 %all-gather.4 = f32[2,1,128]{2,1,0:T(1,128)S(1)} all-gather(f32[1,1,128]{2,1,0:T(1,128)S(1)} %get-tuple-element.174), channel_id=1, replica_groups=mesh['batch'=16,'rep'=2] {'rep'}, dimensions={0}, use_global_device_ids=true | all-gather | bytes 1536 | tf_op jit(solution)/shard_map/all_gather | solution.py:12
  103.1 4.2 %all-gather.3 = f32[2,1,128]{2,1,0:T(1,128)S(1)} all-gather(f32[1,1,128]{2,1,0:T(1,128)S(1)} %get-tuple-element.173), channel_id=2, replica_groups=mesh['batch'=16,'rep'=2] {'rep'}, dimensions={0}, use_global_device_ids=true | all-gather | bytes 1536 | tf_op jit(solution)/shard_map/all_gather | solution.py:12
  107.4 18.8 %all-gather.5 = f32[16,1,128]{2,1,0:T(1,128)S(1)} all-gather(f32[1,1,128]{2,1,0:T(1,128)S(1)} %add_bitcast_fusion.1), channel_id=1, replica_groups=mesh['batch'=16,'rep'=2] {'batch'}, dimensions={0}, use_global_device_ids=true | all-gather | bytes 8704 | tf_op jit(solution)/shard_map/all_gather | solution.py:112
  126.2 0.1 dynamic_slice.58
  126.3 0.0 copy-done
  126.3 1.4 convolution_multiply_fusion.3
  127.7 0.0 reduce-scatter.3.cloned.1.call-update
  127.8 0.0 reduce-scatter.5.cloned.1.call-start
  127.8 0.1 constant_dynamic-slice_fusion.3
  127.9 0.1 eq.35
  128.0 0.1 reshape.71
  128.0 0.1 dynamic-slice_reduce_fusion
  128.1 0.1 sub.117
  128.2 0.1 dynamic_slice.63
  128.3 0.0 all-gather.11.cloned.1.call-done
  128.3 3.1 %convolution_multiply_fusion.2 = f32[128,512]{1,0:T(8,128)} fusion(bf16[1024,512]{1,0:T(8,128)(2,1)} %all-gather.11.cloned.1.call-done, bf16[128,512]{1,0:T(8,128)(2,1)S(1)} %all_gather.39, s32[128]{0:T(128)S(1)} %iota_add_fusion, f32[1024]{0:T(1024)S(1)} %sub.117, f32[128]{0:T(128)S(1)} %dynamic_slice.63, s32[1024]{0:T(1024)S(1)} %eq.35), kind=kOutput, calls=%fused_computation.5 | convolution fusion | flops 269549568 | bytes 1451008 | tf_op jit(solution)/shard_map/dot_general | solution.py:64
  131.4 0.0 reduce-scatter.5.cloned.1.call-update
  131.4 5.5 %reduce-scatter.3.cloned.1.call-done = f32[128,256]{1,0:T(8,128)} async-done(((f32[128,512]{1,0:T(8,128)}), f32[128,256]{1,0:T(8,128)}) %reduce-scatter.3.cloned.1.call-update) | async-done | bytes 131088 | tf_op jit(solution)/shard_map/reduce_scatter | solution.py:173
  136.9 14.5 %reduce-scatter.5.cloned.1.call-done = f32[128,256]{1,0:T(8,128)} async-done(((f32[128,512]{1,0:T(8,128)}), f32[128,256]{1,0:T(8,128)}) %reduce-scatter.5.cloned.1.call-update) | async-done | bytes 131088 | tf_op jit(solution)/shard_map/reduce_scatter | solution.py:174
  (41 shorter events, 0.5 us)
Async XLA Ops:
  7.2 46.6 %all-gather.9.cloned.1.call-start = ((), (), s32[]{:S(2)}) async-start(), calls=%async_computation.2 | async-start | bytes 1114112 | tf_op jit(solution)/shard_map/all_gather | solution.py:167
  14.0 0.8 copy-start.1
  14.0 114.3 %all-gather.11.cloned.1.call-start = ((), (), s32[]{:S(2)}) async-start(), calls=%async_computation.4 | async-start | bytes 1114112 | tf_op jit(solution)/shard_map/all_gather | solution.py:168
  20.4 116.5 %reduce-scatter.3.cloned.1.call-start = ((), (), s32[]{:S(2)}) async-start(), calls=%async_computation.3 | async-start | bytes 393216 | tf_op jit(solution)/shard_map/reduce_scatter | solution.py:173
  20.5 0.7 copy-start.2
  55.5 70.8 %copy-start = (bf16[1024,512]{1,0:T(8,128)(2,1)S(1)}, bf16[1024,512]{1,0:T(8,128)(2,1)}, u32[]{:S(2)}) copy-start(bf16[1024,512]{1,0:T(8,128)(2,1)} %all-gather.9.cloned.1.call-done) | copy-start | bytes 3145732
  127.8 23.6 %reduce-scatter.5.cloned.1.call-start = ((), (), s32[]{:S(2)}) async-start(), calls=%async_computation.5 | async-start | bytes 393216 | tf_op jit(solution)/shard_map/reduce_scatter | solution.py:174
Sparse Core Ops, SparseCore 0:
  14.1 39.5 all-gather.8
  56.5 36.8 all-gather.10
  127.9 8.9 reduce-scatter.2
  139.6 11.7 reduce-scatter.4
where the time goes:
time: 158 us
  blocking collectives  80.1 us (51%)
  waiting for transfers between devices  52.5 us (33%)
  between operations  13.8 us (9%)
  matrix products  6.28 us (4%)
  local copies, waits for them, and re-layouts  3.92 us (2%)
    all_gather x4, blocking collectives, joined(): everything = jax.tree.map(lambda part: lax.all_gather(part, axis), x)  45.8 us
    all_gather x1, waiting for transfers between devices, local(): lax.all_gather(passage_half, 'batch', axis=0, tiled=True)  32.5 us
    all_gather x1, blocking collectives, local(): lax.all_gather(row_high + jnp.log(row_total), 'batch', axis=0, tiled=True)  18.8 us
    reduce_scatter x1, waiting for transfers between devices, local(): lax.psum_scatter(passage_sum * logit_scale, 'rep', scatter_dimension=1, t...  14.5 us
    all_gather x1, blocking collectives, local(): lax.all_gather(passages, 'rep', axis=1, tiled=True)  6.14 us
    reduce_scatter x1, waiting for transfers between devices, local(): lax.psum_scatter(query_sum * logit_scale, 'rep', scatter_dimension=1, til...  5.49 us
    all_gather x1, blocking collectives, local(): lax.all_gather(queries, 'rep', axis=1, tiled=True)  4.92 us
    dot_general x2, matrix products, weighted_sum(): jnp.dot(weights.astype(jnp.bfloat16), remote_set, preferred_element_type=...  4.55 us
  transfers between devices with their start and end apart: 4, of which 3 were waited for; matrix products, arithmetic and copies ran while one was open for 6% of the time, Pallas kernels for 0%

commit v1 on v0

v1 whole, which is shorter than its diff:
```python
import functools
import math

import jax
import jax.numpy as jnp
from jax import lax
from jax.experimental import pallas as pl
from jax.experimental.pallas import tpu as pltpu
from jax.sharding import PartitionSpec as P

MESH = pl.DeviceIdType.MESH
F32 = jnp.float32
BF16 = jnp.bfloat16


def dot(a, b, da, db):
    return lax.dot_general(a, b, (((da,), (db,)), ((), ())), preferred_element_type=F32)


def as_column(row, lanes):
    return jnp.broadcast_to(row, (lanes, row.shape[1])).T


def kernel(
    Z,
    scale,
    q_ref,
    p_ref,
    pos_ref,
    gq_ref,
    gp_ref,
    Q,
    Qs,
    PB,
    S,
    W,
    Ws,
    rst,
    rrc,
    cst,
    crc,
    gqp,
    gqr,
    gpp,
    gpr,
    q_s,
    q_r,
    p_s,
    p_r,
    f_s,
    f_r,
    h_s,
    h_r,
    r_s,
    r_r,
    c_s,
    c_r,
    w_s,
    w_r,
    gq_s,
    gq_r,
    gp_s,
    gp_r,
):
    n, w = q_ref.shape
    b = lax.axis_index("batch")
    x = lax.axis_index("rep")
    z, y, c = b // 4, (b // 2) % 2, b % 2
    rows, cols = 2 * n, Z * n
    blocks = min(Z, 4)
    wide = blocks * n
    chunks = Z // blocks

    def dev(zz, yy, cc, xx):
        return (zz * 4 + yy * 2 + cc, xx)

    def plane(j):
        xx = 1 - x if j & 1 else x
        yy = 1 - y if j & 2 else y
        return xx, yy

    def remote(src, dst, s, r, device):
        return pltpu.make_async_remote_copy(
            src_ref=src, dst_ref=dst, send_sem=s, recv_sem=r, device_id=device, device_id_type=MESH
        )

    def up(dz):
        return (z + dz) % Z

    def down(dz):
        return (z + Z - dz) % Z

    own = c == x
    sibling = dev(z, y, 1 - c, x)

    barrier = pltpu.get_barrier_semaphore()

    def greet(device):
        pl.semaphore_signal(barrier, inc=1, device_id=device, device_id_type=MESH)

    for j in (1, 2, 3):
        xx, yy = plane(j)
        greet(dev(z, yy, c, xx))
    for dz in range(Z):
        if dz:
            greet(dev(up(dz), y, c, x))
            greet(dev(up(dz), y, x, c))
        else:

            @pl.when(jnp.logical_not(own))
            def _():
                greet(dev(z, y, x, c))

        greet(dev(up(dz), y, 1 - c, x))
    Q[x, pl.ds(pl.multiple_of(y * n, n), n), :] = q_ref[...]

    @pl.when(own)
    def _():
        PB[c, pl.ds(pl.multiple_of(z * n, n), n), :] = p_ref[...]

    pl.semaphore_wait(barrier, 3 + 3 * Z - 1 - own.astype(jnp.int32))

    def p_copy(dz, dst_z):
        return remote(
            p_ref,
            PB.at[x, pl.ds(pl.multiple_of(dst_z * n, n), n)],
            p_s.at[dz],
            p_r.at[dz],
            dev(up(dz), y, x, c),
        )

    def q_copy(j):
        xx, yy = plane(j)
        return remote(
            q_ref,
            Q.at[x, pl.ds(pl.multiple_of(y * n, n), n)],
            q_s.at[j - 1],
            q_r.at[j - 1],
            dev(z, yy, c, xx),
        )

    p_copies = [p_copy(dz, z) for dz in range(Z)]
    q_copies = [q_copy(j) for j in (1, 2, 3)]
    forward0 = remote(
        p_ref,
        PB.at[c, pl.ds(pl.multiple_of(z * n, n), n)],
        f_s.at[0],
        f_r.at[0],
        sibling,
    )

    @pl.when(jnp.logical_not(own))
    def _():
        p_copies[0].start()

    @pl.when(own)
    def _():
        forward0.start()

    order = list(range(1, Z))
    for dz in order:
        p_copies[dz].start()
    for copy in q_copies:
        copy.start()

    def forward(dz):
        zs = down(dz)
        part = PB.at[c, pl.ds(pl.multiple_of(zs * n, n), n)]
        return remote(part, part, f_s.at[dz], f_r.at[dz], sibling)

    forwards = [forward(dz) for dz in range(Z)]

    for copy in q_copies:
        copy.wait_recv()
    half = remote(Q.at[1 - c], Qs, h_s, h_r, sibling)
    half.start()

    @pl.when(jnp.logical_not(own))
    def _():
        p_copies[0].wait_recv()
        forwards[0].start()

    for dz in order:
        p_copies[dz].wait_recv()
        forwards[dz].start()
    for dz in range(Z):
        forwards[dz].wait_recv()

    def span(k, size):
        return pl.ds(k * size if isinstance(k, int) else pl.multiple_of(k * size, size), size)

    def score(k, running):
        high, total = running
        at = span(k, wide)
        s = (dot(Q[0], PB[0, at, :], 1, 1) + dot(Q[1], PB[1, at, :], 1, 1)) * scale
        S[:, at] = s
        top = jnp.max(s, axis=0, keepdims=True)
        cst[:, at] = top
        cst[:, span(k + chunks, wide)] = jnp.sum(jnp.exp(s - top), axis=0, keepdims=True)
        new = jnp.maximum(high, jnp.max(s, axis=1, keepdims=True))
        total = total * jnp.exp(high - new) + jnp.sum(jnp.exp(s - new), axis=1, keepdims=True)
        return new, total

    running = (jnp.full((rows, 1), -1e30, F32), jnp.zeros((rows, 1), F32))
    if chunks == 1:
        running = score(0, running)
    else:
        running = lax.fori_loop(0, chunks, score, running)

    col_copies = []
    for dz in range(Z):
        for dc in (0, 1):
            if dz or dc:
                k = dz * 2 + dc
                col_copies.append(
                    remote(
                        cst,
                        crc.at[k],
                        c_s.at[k],
                        c_r.at[k],
                        dev(up(dz), y, 1 - c if dc else c, x),
                    )
                )
                col_copies[-1].start()

    def as_row(column):
        return jnp.broadcast_to(column, (rows, 128)).T[0:1, :]

    rst[:, 0:rows] = as_row(running[0])
    rst[:, rows : 2 * rows] = as_row(running[1])
    row_copies = []
    for j in (1, 2, 3):
        xx, yy = plane(j)
        row_copies.append(
            remote(rst, rrc.at[j], r_s.at[j - 1], r_r.at[j - 1], dev(z, yy, c, xx))
        )
        row_copies[-1].start()

    places = jnp.concatenate(
        [
            as_column(pos_ref[pl.ds(z * 4 + yy * 2 + c, 1), :].astype(F32), 128)
            for yy in (0, 1)
        ],
        axis=0,
    )

    for copy in row_copies:
        copy.wait_recv()
    high = rst[:, 0:rows]
    for j in (1, 2, 3):
        high = jnp.maximum(high, rrc[j, :, 0:rows])
    total = rst[:, rows : 2 * rows] * jnp.exp(rst[:, 0:rows] - high)
    for j in (1, 2, 3):
        total += rrc[j, :, rows : 2 * rows] * jnp.exp(rrc[j, :, 0:rows] - high)
    row_norm = as_column(high + jnp.log(total), 128)

    for copy in col_copies:
        copy.wait_recv()
    high = cst[:, 0:cols]
    for k in range(1, 2 * Z):
        high = jnp.maximum(high, crc[k, :, 0:cols])
    total = cst[:, cols : 2 * cols] * jnp.exp(cst[:, 0:cols] - high)
    for k in range(1, 2 * Z):
        total += crc[k, :, cols : 2 * cols] * jnp.exp(crc[k, :, 0:cols] - high)
    crc[0, :, 0:cols] = high + jnp.log(total)

    lane = lax.broadcasted_iota(jnp.int32, (rows, n), 1).astype(F32)

    def weigh(k, carry):
        at = span(k, n)
        s = S[:, at]
        col_norm = crc[0, :, at]
        base = (k * 4 + y * 2 + x) * n
        hit = jnp.where(places - lane == lax.convert_element_type(base, F32), 2.0, 0.0)
        W[:, at] = (jnp.exp(s - row_norm) + jnp.exp(s - col_norm) - hit).astype(BF16)
        return carry

    if chunks == 1:
        for k in range(Z):
            weigh(k, 0)
    else:
        lax.fori_loop(0, Z, weigh, 0)
    share = remote(W, Ws, w_s, w_r, sibling)
    share.start()

    if chunks == 1:
        for h in (0, 1):
            gqp[h] = dot(W[...], PB[h], 1, 0)
    else:
        gqp[...] = jnp.zeros_like(gqp)

        def gather_terms(k, carry):
            at = span(k, wide)
            for h in (0, 1):
                gqp[h] += dot(W[:, at], PB[h, at, :], 1, 0)
            return carry

        lax.fori_loop(0, chunks, gather_terms, 0)
    gq_copies = []
    for j in (1, 2, 3):
        xx, yy = plane(j)
        gq_copies.append(
            remote(
                gqp.at[xx, pl.ds(pl.multiple_of(yy * n, n), n)],
                gqr.at[j - 1],
                gq_s.at[j - 1],
                gq_r.at[j - 1],
                dev(z, yy, c, xx),
            )
        )
        gq_copies[-1].start()

    half.wait_recv()
    share.wait_recv()

    def passage_terms(k, carry):
        at = span(k, wide)
        gpp[at, :] = dot(W[:, at], Q[c], 0, 0) + dot(Ws[:, at], Qs[...], 0, 0)
        return carry

    if chunks == 1:
        passage_terms(0, 0)
    else:
        lax.fori_loop(0, chunks, passage_terms, 0)

    def gp_copy(dz):
        return remote(
            gpp.at[pl.ds(pl.multiple_of(up(dz) * n, n), n)],
            gpr.at[dz],
            gp_s.at[dz],
            gp_r.at[dz],
            dev(up(dz), y, x, c),
        )

    gp_copies = [gp_copy(dz) for dz in range(Z)]
    for dz in order:
        gp_copies[dz].start()

    @pl.when(jnp.logical_not(own))
    def _():
        gp_copies[0].start()

    for copy in gq_copies:
        copy.wait_recv()
    total = gqp[x, pl.ds(pl.multiple_of(y * n, n), n), :]
    for j in range(3):
        total += gqr[j]
    gq_ref[...] = total * scale

    @pl.when(own)
    def _():
        gpr[0] = gpp[pl.ds(pl.multiple_of(z * n, n), n), :]

    @pl.when(jnp.logical_not(own))
    def _():
        gp_copies[0].wait_recv()

    for dz in order:
        gp_copies[dz].wait_recv()
    total = gpr[0]
    for dz in range(1, Z):
        total += gpr[dz]
    gp_ref[...] = total * scale

    @pl.when(jnp.logical_not(own))
    def _():
        p_copies[0].wait_send()
        gp_copies[0].wait_send()

    for dz in order:
        p_copies[dz].wait_send()
        gp_copies[dz].wait_send()
    for copy in q_copies + forwards + [half, share] + col_copies + row_copies + gq_copies:
        copy.wait_send()


def local(queries, passages, positives):
    n, w = queries.shape
    batch_count = lax.axis_size("batch")
    Z = batch_count // 4
    scale = 1.0 / math.sqrt(w * lax.axis_size("rep"))
    rows, cols = 2 * n, Z * n
    vmem = pl.BlockSpec(memory_space=pltpu.VMEM)
    dma = pltpu.SemaphoreType.DMA
    return pl.pallas_call(
        functools.partial(kernel, Z, scale),
        out_shape=(
            jax.ShapeDtypeStruct((n, w), F32),
            jax.ShapeDtypeStruct((n, w), F32),
        ),
        in_specs=[vmem] * 3,
        out_specs=(vmem, vmem),
        scratch_shapes=[
            pltpu.VMEM((2, rows, w), BF16),
            pltpu.VMEM((rows, w), BF16),
            pltpu.VMEM((2, cols, w), BF16),
            pltpu.VMEM((rows, cols), F32),
            pltpu.VMEM((rows, cols), BF16),
            pltpu.VMEM((rows, cols), BF16),
            pltpu.VMEM((1, 2 * rows), F32),
            pltpu.VMEM((4, 1, 2 * rows), F32),
            pltpu.VMEM((1, 2 * cols), F32),
            pltpu.VMEM((2 * Z, 1, 2 * cols), F32),
            pltpu.VMEM((2, rows, w), F32),
            pltpu.VMEM((3, n, w), F32),
            pltpu.VMEM((cols, w), F32),
            pltpu.VMEM((Z, n, w), F32),
            dma((3,)),
            dma((3,)),
            dma((Z,)),
            dma((Z,)),
            dma((Z,)),
            dma((Z,)),
            dma,
            dma,
            dma((3,)),
            dma((3,)),
            dma((2 * Z,)),
            dma((2 * Z,)),
            dma,
            dma,
            dma((3,)),
            dma((3,)),
            dma((Z,)),
            dma((Z,)),
        ],
        compiler_params=pltpu.CompilerParams(collective_id=0, has_side_effects=True),
    )(queries, passages, positives.reshape(batch_count, n))


def solution(mesh):
    in_specs = (P("batch", "rep"), P("batch", "rep"), P())
    out_specs = (P("batch", "rep"), P("batch", "rep"))
    return jax.shard_map(local, mesh=mesh, in_specs=in_specs, out_specs=out_specs, check_vma=False)
```

time: 158 us -> 37.9 us (0.24)
  the two profiles are of different devices: /device:TPU:0 before, /device:TPU:9 now
where the time goes in v1:
time: 37.9 us; the launch traced here: 37.7 us
  Pallas kernels  34.8 us (92%)
  local copies, waits for them, and re-layouts  2.26 us (6%)
  between operations  0.65 us (2%)
    pallas_call x1, Pallas kernels, local(): pl.pallas_call(functools.partial(kernel, Z, scale), out_shape=(jax.ShapeD...  34.8 us
    unnamed x4, local copies, waits for them, and re-layouts  2.26 us

profile of v1, /device:TPU:9, one launch (start us, length us, event | category | flops | bytes accessed | tf_op | source)
XLA Modules:
  0.0 37.7 jit_solution(5955145106498132939)
XLA Ops:
  0.6 34.8 %shard_map.50 = (f32[128,256]{1,0:T(8,128)}, f32[128,256]{1,0:T(8,128)}) custom-call(bf16[128,256]{1,0:T(8,128)(2,1)} %q_ref.1, bf16[128,256]{1,0:T(8,128)(2,1)} %p_ref.1, s32[16,128]{1,0:T(8,128)} %bitcast.1), custom_call_target="tpu_custom_call" | custom-call | tf_op jit(solution)/shard_map/pallas_call | solution.py:385
  35.4 0.0 copy-start
  35.4 1.6 %copy.7 = f32[128,256]{1,0:T(8,128)} copy(f32[128,256]{1,0:T(8,128)} %get-tuple-element.4) | data formatting | bytes 262144
  37.0 0.0 copy-done
  37.0 0.7 %copy.8 = f32[128,256]{1,0:T(8,128)} copy(f32[128,256]{1,0:T(8,128)S(1)} %copy-done) | data formatting | bytes 262144
Async XLA Ops:
  35.4 1.6 %copy-start = (f32[128,256]{1,0:T(8,128)S(1)}, f32[128,256]{1,0:T(8,128)}, u32[]{:S(2)}) copy-start(f32[128,256]{1,0:T(8,128)} %get-tuple-element.5) | copy-start | bytes 393220

commit v2 on v1

--- a/solution.py
+++ b/solution.py
@@ -11,6 +11,7 @@
 MESH = pl.DeviceIdType.MESH
 F32 = jnp.float32
 BF16 = jnp.bfloat16
+I16 = jnp.int16
 
 
 def dot(a, b, da, db):
@@ -39,10 +40,18 @@
     rrc,
     cst,
     crc,
+    PM,
     gqp,
+    gqt,
     gqr,
+    gqk,
+    gqkr,
     gpp,
+    gpt,
     gpr,
+    gpk,
+    gpkr,
+    fin,
     q_s,
     q_r,
     p_s,
@@ -61,6 +70,11 @@
     gq_r,
     gp_s,
     gp_r,
+    gqk_s,
+    gqk_r,
+    gpk_s,
+    gpk_r,
+    in_s,
 ):
     n, w = q_ref.shape
     b = lax.axis_index("batch")
@@ -95,6 +109,12 @@
 
     barrier = pltpu.get_barrier_semaphore()
 
+    q_own = Q.at[x, pl.ds(pl.multiple_of(y * n, n), n)]
+    p_in = pltpu.make_async_copy(p_ref, PM, in_s.at[0])
+    q_in = pltpu.make_async_copy(q_ref, q_own, in_s.at[1])
+    p_in.start()
+    q_in.start()
+
     def greet(device):
         pl.semaphore_signal(barrier, inc=1, device_id=device, device_id_type=MESH)
 
@@ -112,17 +132,18 @@
                 greet(dev(z, y, x, c))
 
         greet(dev(up(dz), y, 1 - c, x))
-    Q[x, pl.ds(pl.multiple_of(y * n, n), n), :] = q_ref[...]
+    p_in.wait()
+    q_in.wait()
 
     @pl.when(own)
     def _():
-        PB[c, pl.ds(pl.multiple_of(z * n, n), n), :] = p_ref[...]
+        PB[c, pl.ds(pl.multiple_of(z * n, n), n), :] = PM[...]
 
     pl.semaphore_wait(barrier, 3 + 3 * Z - 1 - own.astype(jnp.int32))
 
     def p_copy(dz, dst_z):
         return remote(
-            p_ref,
+            PM,
             PB.at[x, pl.ds(pl.multiple_of(dst_z * n, n), n)],
             p_s.at[dz],
             p_r.at[dz],
@@ -132,8 +153,8 @@
     def q_copy(j):
         xx, yy = plane(j)
         return remote(
-            q_ref,
-            Q.at[x, pl.ds(pl.multiple_of(y * n, n), n)],
+            q_own,
+            q_own,
             q_s.at[j - 1],
             q_r.at[j - 1],
             dev(z, yy, c, xx),
@@ -142,7 +163,7 @@
     p_copies = [p_copy(dz, z) for dz in range(Z)]
     q_copies = [q_copy(j) for j in (1, 2, 3)]
     forward0 = remote(
-        p_ref,
+        PM,
         PB.at[c, pl.ds(pl.multiple_of(z * n, n), n)],
         f_s.at[0],
         f_r.at[0],
@@ -283,6 +304,14 @@
     share = remote(W, Ws, w_s, w_r, sibling)
     share.start()
 
+    def pack(value, to, step, k):
+        top = jnp.maximum(jnp.max(jnp.abs(value), axis=0, keepdims=True), 1e-30)
+        to[k] = jnp.round(value * (32766.0 / top)).astype(jnp.int32).astype(I16)
+        step[k] = top * (1.0 / 32766.0)
+
+    def unpack(at, step, k):
+        return at[k].astype(jnp.int32).astype(F32) * step[k]
+
     if chunks == 1:
         for h in (0, 1):
             gqp[h] = dot(W[...], PB[h], 1, 0)
@@ -297,18 +326,20 @@
 
         lax.fori_loop(0, chunks, gather_terms, 0)
     gq_copies = []
-    for j in (1, 2, 3):
+    for j in (3, 1, 2):
         xx, yy = plane(j)
-        gq_copies.append(
-            remote(
-                gqp.at[xx, pl.ds(pl.multiple_of(yy * n, n), n)],
-                gqr.at[j - 1],
-                gq_s.at[j - 1],
-                gq_r.at[j - 1],
-                dev(z, yy, c, xx),
+        pack(gqp[xx, pl.ds(pl.multiple_of(yy * n, n), n), :], gqt, gqk, j - 1)
+        for src, dst, ss, rr in ((gqt, gqr, gq_s, gq_r), (gqk, gqkr, gqk_s, gqk_r)):
+            gq_copies.append(
+                remote(
+                    src.at[j - 1],
+                    dst.at[j - 1],
+                    ss.at[j - 1],
+                    rr.at[j - 1],
+                    dev(z, yy, c, xx),
+                )
             )
-        )
-        gq_copies[-1].start()
+            gq_copies[-1].start()
 
     half.wait_recv()
     share.wait_recv()
@@ -324,52 +355,62 @@
         lax.fori_loop(0, chunks, passage_terms, 0)
 
     def gp_copy(dz):
-        return remote(
-            gpp.at[pl.ds(pl.multiple_of(up(dz) * n, n), n)],
-            gpr.at[dz],
-            gp_s.at[dz],
-            gp_r.at[dz],
-            dev(up(dz), y, x, c),
+        device = dev(up(dz), y, x, c)
+        return (
+            remote(gpt.at[dz], gpr.at[dz], gp_s.at[dz], gp_r.at[dz], device),
+            remote(gpk.at[dz], gpkr.at[dz], gpk_s.at[dz], gpk_r.at[dz], device),
         )
 
     gp_copies = [gp_copy(dz) for dz in range(Z)]
+
+    def gp_send(dz):
+        at = pl.ds(pl.multiple_of(up(dz) * n, n), n)
+        pack(gpp[at, :], gpt, gpk, dz)
+        for copy in gp_copies[dz]:
+            copy.start()
+
     for dz in order:
-        gp_copies[dz].start()
+        gp_send(dz)
 
     @pl.when(jnp.logical_not(own))
     def _():
-        gp_copies[0].start()
+        gp_send(0)
+
+    @pl.when(own)
+    def _():
+        fin[...] = gpp[pl.ds(pl.multiple_of(z * n, n), n), :]
 
     for copy in gq_copies:
         copy.wait_recv()
     total = gqp[x, pl.ds(pl.multiple_of(y * n, n), n), :]
     for j in range(3):
-        total += gqr[j]
-    gq_ref[...] = total * scale
-
-    @pl.when(own)
-    def _():
-        gpr[0] = gpp[pl.ds(pl.multiple_of(z * n, n), n), :]
+        total += unpack(gqr, gqkr, j)
+    gq_ref[...] = total
 
     @pl.when(jnp.logical_not(own))
     def _():
-        gp_copies[0].wait_recv()
+        for copy in gp_copies[0]:
+            copy.wait_recv()
+        fin[...] = unpack(gpr, gpkr, 0)
 
     for dz in order:
-        gp_copies[dz].wait_recv()
-    total = gpr[0]
+        for copy in gp_copies[dz]:
+            copy.wait_recv()
+    total = fin[...]
     for dz in range(1, Z):
-        total += gpr[dz]
-    gp_ref[...] = total * scale
+        total += unpack(gpr, gpkr, dz)
+    gp_ref[...] = total
 
     @pl.when(jnp.logical_not(own))
     def _():
         p_copies[0].wait_send()
-        gp_copies[0].wait_send()
+        for copy in gp_copies[0]:
+            copy.wait_send()
 
     for dz in order:
         p_copies[dz].wait_send()
-        gp_copies[dz].wait_send()
+        for copy in gp_copies[dz]:
+            copy.wait_send()
     for copy in q_copies + forwards + [half, share] + col_copies + row_copies + gq_copies:
         copy.wait_send()
 
@@ -382,13 +423,14 @@
     rows, cols = 2 * n, Z * n
     vmem = pl.BlockSpec(memory_space=pltpu.VMEM)
     dma = pltpu.SemaphoreType.DMA
-    return pl.pallas_call(
+    hbm = pl.BlockSpec(memory_space=pltpu.HBM)
+    grad_queries, grad_passages = pl.pallas_call(
         functools.partial(kernel, Z, scale),
         out_shape=(
             jax.ShapeDtypeStruct((n, w), F32),
             jax.ShapeDtypeStruct((n, w), F32),
         ),
-        in_specs=[vmem] * 3,
+        in_specs=[hbm, hbm, vmem],
         out_specs=(vmem, vmem),
         scratch_shapes=[
             pltpu.VMEM((2, rows, w), BF16),
@@ -401,10 +443,18 @@
             pltpu.VMEM((4, 1, 2 * rows), F32),
             pltpu.VMEM((1, 2 * cols), F32),
             pltpu.VMEM((2 * Z, 1, 2 * cols), F32),
+            pltpu.VMEM((n, w), BF16),
             pltpu.VMEM((2, rows, w), F32),
-            pltpu.VMEM((3, n, w), F32),
+            pltpu.VMEM((3, n, w), I16),
+            pltpu.VMEM((3, n, w), I16),
+            pltpu.VMEM((3, 1, w), F32),
+            pltpu.VMEM((3, 1, w), F32),
             pltpu.VMEM((cols, w), F32),
-            pltpu.VMEM((Z, n, w), F32),
+            pltpu.VMEM((Z, n, w), I16),
+            pltpu.VMEM((Z, n, w), I16),
+            pltpu.VMEM((Z, 1, w), F32),
+            pltpu.VMEM((Z, 1, w), F32),
+            pltpu.VMEM((n, w), F32),
             dma((3,)),
             dma((3,)),
             dma((Z,)),
@@ -423,9 +473,15 @@
             dma((3,)),
             dma((Z,)),
             dma((Z,)),
+            dma((3,)),
+            dma((3,)),
+            dma((Z,)),
+            dma((Z,)),
+            dma((2,)),
         ],
-        compiler_params=pltpu.CompilerParams(collective_id=0, has_side_effects=True),
-    )(queries, passages, positives.reshape(batch_count, n))
+        compiler_params=pltpu.CompilerParams(collective_id=0, has_side_effects=True, vmem_limit_bytes=6 * 2**20 + 40 * rows * cols),
+    )(pltpu.with_memory_space_constraint(queries, pltpu.HBM), pltpu.with_memory_space_constraint(passages, pltpu.HBM), positives.reshape(batch_count, n))
+    return grad_queries * scale, grad_passages * scale
 
 
 def solution(mesh):

time: 37.9 us -> 30.9 us (0.82)
  the two profiles are of different devices: /device:TPU:9 before, /device:TPU:0 now
where the time goes in v2:
time: 30.9 us; the launch traced here: 30.5 us
  Pallas kernels  28.4 us (92%)
  other arithmetic  0.72 us (2%)
  local copies, waits for them, and re-layouts  0.69 us (2%)
  between operations  0.65 us (2%)
    pallas_call x1, Pallas kernels, local(): pl.pallas_call(functools.partial(kernel, Z, scale), out_shape=(jax.ShapeD...  28.4 us
    mul x1, other arithmetic, local(): return (grad_queries * scale, grad_passages * scale)  0.72 us
    unnamed x2, local copies, waits for them, and re-layouts  0.69 us

profile of v2, /device:TPU:0, one launch (start us, length us, event | category | flops | bytes accessed | tf_op | source)
XLA Modules:
  0.0 30.5 jit_solution(3318799317361296462)
XLA Ops:
  0.6 0.0 copy-start
  0.6 0.7 %copy-done = s32[2048]{0:T(1024)S(1)} copy-done((s32[2048]{0:T(1024)S(1)}, s32[2048]{0:T(1024)}, u32[]{:S(2)}) %copy-start) | copy-done | bytes 8216
  1.3 28.4 %shard_map.50 = (f32[128,256]{1,0:T(8,128)S(1)}, f32[128,256]{1,0:T(8,128)S(1)}) custom-call(bf16[128,256]{1,0:T(8,128)(2,1)} %q_ref.1, bf16[128,256]{1,0:T(8,128)(2,1)} %p_ref.1, s32[16,128]{1,0:T(8,128)S(1)} %bitcast.1), custom_call_target="tpu_custom_call" | custom-call | tf_op jit(solution)/shard_map/pallas_call | solution.py:427
  29.8 0.7 %broadcast_multiply_fusion = (f32[128,256]{1,0:T(8,128)}, f32[128,256]{1,0:T(8,128)}) fusion(f32[128,256]{1,0:T(8,128)S(1)} %get-tuple-element.5, f32[128,256]{1,0:T(8,128)S(1)} %get-tuple-element.4), kind=kLoop, calls=%fused_computation | loop fusion | flops 65536 | bytes 524288 | tf_op jit(solution)/shard_map/mul | solution.py:484
Async XLA Ops:
  0.6 0.7 %copy-start = (s32[2048]{0:T(1024)S(1)}, s32[2048]{0:T(1024)}, u32[]{:S(2)}) copy-start(s32[2048]{0:T(1024)} %param.5) | copy-start | bytes 24580

commit v3 on v2

--- a/solution.py
+++ b/solution.py
@@ -27,7 +27,7 @@
     scale,
     q_ref,
     p_ref,
-    pos_ref,
+    pos_hbm,
     gq_ref,
     gp_ref,
     Q,
@@ -41,12 +41,12 @@
     cst,
     crc,
     PM,
+    pos_ref,
     gqp,
     gqt,
     gqr,
     gqk,
     gqkr,
-    gpp,
     gpt,
     gpr,
     gpk,
@@ -112,8 +112,10 @@
     q_own = Q.at[x, pl.ds(pl.multiple_of(y * n, n), n)]
     p_in = pltpu.make_async_copy(p_ref, PM, in_s.at[0])
     q_in = pltpu.make_async_copy(q_ref, q_own, in_s.at[1])
+    pos_in = pltpu.make_async_copy(pos_hbm, pos_ref, in_s.at[2])
     p_in.start()
     q_in.start()
+    pos_in.start()
 
     def greet(device):
         pl.semaphore_signal(barrier, inc=1, device_id=device, device_id_type=MESH)
@@ -134,6 +136,7 @@
         greet(dev(up(dz), y, 1 - c, x))
     p_in.wait()
     q_in.wait()
+    pos_in.wait()
 
     @pl.when(own)
     def _():
@@ -141,13 +144,17 @@
 
     pl.semaphore_wait(barrier, 3 + 3 * Z - 1 - own.astype(jnp.int32))
 
-    def p_copy(dz, dst_z):
+    slot = PB.at[c, pl.ds(pl.multiple_of(z * n, n), n)]
+
+    def p_copy(dz):
+        if dz:
+            return remote(slot, slot, p_s.at[dz], p_r.at[dz], dev(up(dz), y, c, x))
         return remote(
             PM,
-            PB.at[x, pl.ds(pl.multiple_of(dst_z * n, n), n)],
-            p_s.at[dz],
-            p_r.at[dz],
-            dev(up(dz), y, x, c),
+            PB.at[x, pl.ds(pl.multiple_of(z * n, n), n)],
+            p_s.at[0],
+            p_r.at[0],
+            dev(z, y, x, c),
         )
 
     def q_copy(j):
@@ -160,30 +167,8 @@
             dev(z, yy, c, xx),
         )
 
-    p_copies = [p_copy(dz, z) for dz in range(Z)]
+    p_copies = [p_copy(dz) for dz in range(Z)]
     q_copies = [q_copy(j) for j in (1, 2, 3)]
-    forward0 = remote(
-        PM,
-        PB.at[c, pl.ds(pl.multiple_of(z * n, n), n)],
-        f_s.at[0],
-        f_r.at[0],
-        sibling,
-    )
-
-    @pl.when(jnp.logical_not(own))
-    def _():
-        p_copies[0].start()
-
-    @pl.when(own)
-    def _():
-        forward0.start()
-
-    order = list(range(1, Z))
-    for dz in order:
-        p_copies[dz].start()
-    for copy in q_copies:
-        copy.start()
-
     def forward(dz):
         zs = down(dz)
         part = PB.at[c, pl.ds(pl.multiple_of(zs * n, n), n)]
@@ -191,42 +176,44 @@
 
     forwards = [forward(dz) for dz in range(Z)]
 
+    @pl.when(jnp.logical_not(own))
+    def _():
+        p_copies[0].start()
+
+    for copy in q_copies:
+        copy.start()
+
+    @pl.when(jnp.logical_not(own))
+    def _():
+        p_copies[0].wait_recv()
+
+    order = list(range(1, Z))
+    for dz in order:
+        p_copies[dz].start()
+    forwards[0].start()
+
+    def span(k, size):
+        return pl.ds(k * size if isinstance(k, int) else pl.multiple_of(k * size, size), size)
+
+    def score(dz):
+        forwards[dz].wait_recv()
+        zs = down(dz)
+        at = span(zs, n)
+        s = (dot(Q[0], PB[0, at, :], 1, 1) + dot(Q[1], PB[1, at, :], 1, 1)) * scale
+        S[:, at] = s
+        top = jnp.max(s, axis=0, keepdims=True)
+        cst[:, at] = top
+        cst[:, span(zs + Z, n)] = jnp.sum(jnp.exp(s - top), axis=0, keepdims=True)
+
     for copy in q_copies:
         copy.wait_recv()
     half = remote(Q.at[1 - c], Qs, h_s, h_r, sibling)
     half.start()
-
-    @pl.when(jnp.logical_not(own))
-    def _():
-        p_copies[0].wait_recv()
-        forwards[0].start()
-
     for dz in order:
         p_copies[dz].wait_recv()
         forwards[dz].start()
-    for dz in range(Z):
-        forwards[dz].wait_recv()
-
-    def span(k, size):
-        return pl.ds(k * size if isinstance(k, int) else pl.multiple_of(k * size, size), size)
-
-    def score(k, running):
-        high, total = running
-        at = span(k, wide)
-        s = (dot(Q[0], PB[0, at, :], 1, 1) + dot(Q[1], PB[1, at, :], 1, 1)) * scale
-        S[:, at] = s
-        top = jnp.max(s, axis=0, keepdims=True)
-        cst[:, at] = top
-        cst[:, span(k + chunks, wide)] = jnp.sum(jnp.exp(s - top), axis=0, keepdims=True)
-        new = jnp.maximum(high, jnp.max(s, axis=1, keepdims=True))
-        total = total * jnp.exp(high - new) + jnp.sum(jnp.exp(s - new), axis=1, keepdims=True)
-        return new, total
-
-    running = (jnp.full((rows, 1), -1e30, F32), jnp.zeros((rows, 1), F32))
-    if chunks == 1:
-        running = score(0, running)
-    else:
-        running = lax.fori_loop(0, chunks, score, running)
+        score(dz - 1)
+    score(Z - 1)
 
     col_copies = []
     for dz in range(Z):
@@ -244,6 +231,21 @@
                 )
                 col_copies[-1].start()
 
+    def row_high(k, high):
+        return jnp.maximum(high, jnp.max(S[:, span(k, wide)], axis=1, keepdims=True))
+
+    def row_total(k, total):
+        s = S[:, span(k, wide)]
+        return total + jnp.sum(jnp.exp(s - highest), axis=1, keepdims=True)
+
+    low, zero = jnp.full((rows, 1), -1e30, F32), jnp.zeros((rows, 1), F32)
+    if chunks == 1:
+        highest = row_high(0, low)
+        running = (highest, row_total(0, zero))
+    else:
+        highest = lax.fori_loop(0, chunks, row_high, low)
+        running = (highest, lax.fori_loop(0, chunks, row_total, zero))
+
     def as_row(column):
         return jnp.broadcast_to(column, (rows, 128)).T[0:1, :]
 
@@ -287,22 +289,18 @@
 
     lane = lax.broadcasted_iota(jnp.int32, (rows, n), 1).astype(F32)
 
-    def weigh(k, carry):
-        at = span(k, n)
+    shares = []
+    turn = order + [0]
+    for dz in turn:
+        zb = up(dz)
+        at = span(zb, n)
         s = S[:, at]
         col_norm = crc[0, :, at]
-        base = (k * 4 + y * 2 + x) * n
-        hit = jnp.where(places - lane == lax.convert_element_type(base, F32), 2.0, 0.0)
-        W[:, at] = (jnp.exp(s - row_norm) + jnp.exp(s - col_norm) - hit).astype(BF16)
-        return carry
-
-    if chunks == 1:
-        for k in range(Z):
-            weigh(k, 0)
-    else:
-        lax.fori_loop(0, Z, weigh, 0)
-    share = remote(W, Ws, w_s, w_r, sibling)
-    share.start()
+        base = lax.convert_element_type((zb * 4 + y * 2 + x) * n, F32)
+        hit = jnp.where(places - lane == base, 2.0, 0.0)
+        W[dz] = (jnp.exp(s - row_norm) + jnp.exp(s - col_norm) - hit).astype(BF16)
+        shares.append(remote(W.at[dz], Ws.at[dz], w_s.at[dz], w_r.at[dz], sibling))
+        shares[-1].start()
 
     def pack(value, to, step, k):
         top = jnp.maximum(jnp.max(jnp.abs(value), axis=0, keepdims=True), 1e-30)
@@ -312,19 +310,30 @@
     def unpack(at, step, k):
         return at[k].astype(jnp.int32).astype(F32) * step[k]
 
-    if chunks == 1:
-        for h in (0, 1):
-            gqp[h] = dot(W[...], PB[h], 1, 0)
-    else:
-        gqp[...] = jnp.zeros_like(gqp)
-
-        def gather_terms(k, carry):
-            at = span(k, wide)
-            for h in (0, 1):
-                gqp[h] += dot(W[:, at], PB[h, at, :], 1, 0)
-            return carry
-
-        lax.fori_loop(0, chunks, gather_terms, 0)
+    def gp_copy(dz):
+        device = dev(up(dz), y, x, c)
+        return (
+            remote(gpt.at[dz], gpr.at[dz], gp_s.at[dz], gp_r.at[dz], device),
+            remote(gpk.at[dz], gpkr.at[dz], gpk_s.at[dz], gpk_r.at[dz], device),
+        )
+
+    gp_copies = [gp_copy(dz) for dz in range(Z)]
+
+    def gp_send(value, dz):
+        pack(value, gpt, gpk, dz)
+        for copy in gp_copies[dz]:
+            copy.start()
+
+    def query_terms(h):
+        def term(k):
+            return dot(W[k], PB[h, span(up(k), n), :], 1, 0)
+
+        if Z <= 4:
+            return sum(term(k) for k in range(1, Z)) + term(0)
+        return lax.fori_loop(0, Z, lambda k, t: t + term(k), jnp.zeros((rows, w), F32))
+
+    for h in (0, 1):
+        gqp[h] = query_terms(h)
     gq_copies = []
     for j in (3, 1, 2):
         xx, yy = plane(j)
@@ -342,43 +351,17 @@
             gq_copies[-1].start()
 
     half.wait_recv()
-    share.wait_recv()
-
-    def passage_terms(k, carry):
-        at = span(k, wide)
-        gpp[at, :] = dot(W[:, at], Q[c], 0, 0) + dot(Ws[:, at], Qs[...], 0, 0)
-        return carry
-
-    if chunks == 1:
-        passage_terms(0, 0)
-    else:
-        lax.fori_loop(0, chunks, passage_terms, 0)
-
-    def gp_copy(dz):
-        device = dev(up(dz), y, x, c)
-        return (
-            remote(gpt.at[dz], gpr.at[dz], gp_s.at[dz], gp_r.at[dz], device),
-            remote(gpk.at[dz], gpkr.at[dz], gpk_s.at[dz], gpk_r.at[dz], device),
-        )
-
-    gp_copies = [gp_copy(dz) for dz in range(Z)]
-
-    def gp_send(dz):
-        at = pl.ds(pl.multiple_of(up(dz) * n, n), n)
-        pack(gpp[at, :], gpt, gpk, dz)
-        for copy in gp_copies[dz]:
-            copy.start()
-
-    for dz in order:
-        gp_send(dz)
-
-    @pl.when(jnp.logical_not(own))
-    def _():
-        gp_send(0)
-
-    @pl.when(own)
-    def _():
-        fin[...] = gpp[pl.ds(pl.multiple_of(z * n, n), n), :]
+    for dz, share in zip(turn, shares):
+        share.wait_recv()
+        value = dot(W[dz], Q[c], 0, 0) + dot(Ws[dz], Qs[...], 0, 0)
+        if dz:
+            gp_send(value, dz)
+        else:
+            fin[...] = value
+
+            @pl.when(jnp.logical_not(own))
+            def _():
+                gp_send(fin[...], 0)
 
     for copy in gq_copies:
         copy.wait_recv()
@@ -411,7 +394,7 @@
         p_copies[dz].wait_send()
         for copy in gp_copies[dz]:
             copy.wait_send()
-    for copy in q_copies + forwards + [half, share] + col_copies + row_copies + gq_copies:
+    for copy in q_copies + forwards + [half] + shares + col_copies + row_copies + gq_copies:
         copy.wait_send()
 
 
@@ -424,32 +407,33 @@
     vmem = pl.BlockSpec(memory_space=pltpu.VMEM)
     dma = pltpu.SemaphoreType.DMA
     hbm = pl.BlockSpec(memory_space=pltpu.HBM)
+    operands = (queries, passages, positives.reshape(batch_count, n))
     grad_queries, grad_passages = pl.pallas_call(
         functools.partial(kernel, Z, scale),
         out_shape=(
             jax.ShapeDtypeStruct((n, w), F32),
             jax.ShapeDtypeStruct((n, w), F32),
         ),
-        in_specs=[hbm, hbm, vmem],
+        in_specs=[hbm] * 3,
         out_specs=(vmem, vmem),
         scratch_shapes=[
             pltpu.VMEM((2, rows, w), BF16),
             pltpu.VMEM((rows, w), BF16),
             pltpu.VMEM((2, cols, w), BF16),
             pltpu.VMEM((rows, cols), F32),
-            pltpu.VMEM((rows, cols), BF16),
-            pltpu.VMEM((rows, cols), BF16),
+            pltpu.VMEM((Z, rows, n), BF16),
+            pltpu.VMEM((Z, rows, n), BF16),
             pltpu.VMEM((1, 2 * rows), F32),
             pltpu.VMEM((4, 1, 2 * rows), F32),
             pltpu.VMEM((1, 2 * cols), F32),
             pltpu.VMEM((2 * Z, 1, 2 * cols), F32),
             pltpu.VMEM((n, w), BF16),
+            pltpu.VMEM((batch_count, n), jnp.int32),
             pltpu.VMEM((2, rows, w), F32),
             pltpu.VMEM((3, n, w), I16),
             pltpu.VMEM((3, n, w), I16),
             pltpu.VMEM((3, 1, w), F32),
             pltpu.VMEM((3, 1, w), F32),
-            pltpu.VMEM((cols, w), F32),
             pltpu.VMEM((Z, n, w), I16),
             pltpu.VMEM((Z, n, w), I16),
             pltpu.VMEM((Z, 1, w), F32),
@@ -467,20 +451,20 @@
             dma((3,)),
             dma((2 * Z,)),
             dma((2 * Z,)),
-            dma,
-            dma,
-            dma((3,)),
-            dma((3,)),
-            dma((Z,)),
-            dma((Z,)),
-            dma((3,)),
-            dma((3,)),
-            dma((Z,)),
-            dma((Z,)),
-            dma((2,)),
+            dma((Z,)),
+            dma((Z,)),
+            dma((3,)),
+            dma((3,)),
+            dma((Z,)),
+            dma((Z,)),
+            dma((3,)),
+            dma((3,)),
+            dma((Z,)),
+            dma((Z,)),
+            dma((3,)),
         ],
         compiler_params=pltpu.CompilerParams(collective_id=0, has_side_effects=True, vmem_limit_bytes=6 * 2**20 + 40 * rows * cols),
-    )(pltpu.with_memory_space_constraint(queries, pltpu.HBM), pltpu.with_memory_space_constraint(passages, pltpu.HBM), positives.reshape(batch_count, n))
+    )(*(pltpu.with_memory_space_constraint(a, pltpu.HBM) for a in operands))
     return grad_queries * scale, grad_passages * scale
 
 

time: 30.9 us -> 30.2 us (0.977)
  local copies, waits for them, and re-layouts: 0.69 us -> 0 us
    unnamed x2 -> x0, local copies, waits for them, and re-layouts: 0.69 us -> none
where the time goes in v3:
time: 30.2 us; the launch traced here: 30.1 us
  Pallas kernels  28.7 us (95%)
  other arithmetic  0.72 us (2%)
  between operations  0.64 us (2%)
    pallas_call x1, Pallas kernels, local(): pl.pallas_call(functools.partial(kernel, Z, scale), out_shape=(jax.ShapeD...  28.7 us
    mul x1, other arithmetic, local(): return (grad_queries * scale, grad_passages * scale)  0.72 us

profile of v3, /device:TPU:0, one launch (start us, length us, event | category | flops | bytes accessed | tf_op | source)
XLA Modules:
  0.0 30.1 jit_solution(13705910049877134265)
XLA Ops:
  0.6 28.7 %shard_map.50 = (f32[128,256]{1,0:T(8,128)S(1)}, f32[128,256]{1,0:T(8,128)S(1)}) custom-call(bf16[128,256]{1,0:T(8,128)(2,1)} %q_ref.1, bf16[128,256]{1,0:T(8,128)(2,1)} %p_ref.1, s32[16,128]{1,0:T(8,128)} %bitcast.1), custom_call_target="tpu_custom_call" | custom-call | tf_op jit(solution)/shard_map/pallas_call | solution.py:411
  29.4 0.7 %broadcast_multiply_fusion = (f32[128,256]{1,0:T(8,128)}, f32[128,256]{1,0:T(8,128)}) fusion(f32[128,256]{1,0:T(8,128)S(1)} %get-tuple-element.5, f32[128,256]{1,0:T(8,128)S(1)} %get-tuple-element.4), kind=kLoop, calls=%fused_computation | loop fusion | flops 65536 | bytes 524288 | tf_op jit(solution)/shard_map/mul | solution.py:468

commit v4 on v3

--- a/solution.py
+++ b/solution.py
@@ -332,10 +332,11 @@
             return sum(term(k) for k in range(1, Z)) + term(0)
         return lax.fori_loop(0, Z, lambda k, t: t + term(k), jnp.zeros((rows, w), F32))
 
-    for h in (0, 1):
-        gqp[h] = query_terms(h)
+    gqp[1 - x] = query_terms(1 - x)
     gq_copies = []
     for j in (3, 1, 2):
+        if j == 2:
+            gqp[x] = query_terms(x)
         xx, yy = plane(j)
         pack(gqp[xx, pl.ds(pl.multiple_of(yy * n, n), n), :], gqt, gqk, j - 1)
         for src, dst, ss, rr in ((gqt, gqr, gq_s, gq_r), (gqk, gqkr, gqk_s, gqk_r)):

time: 30.2 us -> 30.5 us (level)
  no operation moved by 1% of the time
where the time goes in v4:
time: 30.5 us; the launch traced here: 30.3 us
  Pallas kernels  28.9 us (95%)
  other arithmetic  0.72 us (2%)
  between operations  0.64 us (2%)
    pallas_call x1, Pallas kernels, local(): pl.pallas_call(functools.partial(kernel, Z, scale), out_shape=(jax.ShapeD...  28.9 us
    mul x1, other arithmetic, local(): return (grad_queries * scale, grad_passages * scale)  0.72 us

profile of v4, /device:TPU:0, one launch (start us, length us, event | category | flops | bytes accessed | tf_op | source)
XLA Modules:
  0.0 30.3 jit_solution(2209903659071269794)
XLA Ops:
  0.6 28.9 %shard_map.50 = (f32[128,256]{1,0:T(8,128)S(1)}, f32[128,256]{1,0:T(8,128)S(1)}) custom-call(bf16[128,256]{1,0:T(8,128)(2,1)} %q_ref.1, bf16[128,256]{1,0:T(8,128)(2,1)} %p_ref.1, s32[16,128]{1,0:T(8,128)} %bitcast.1), custom_call_target="tpu_custom_call" | custom-call | tf_op jit(solution)/shard_map/pallas_call | solution.py:412
  29.6 0.7 %broadcast_multiply_fusion = (f32[128,256]{1,0:T(8,128)}, f32[128,256]{1,0:T(8,128)}) fusion(f32[128,256]{1,0:T(8,128)S(1)} %get-tuple-element.5, f32[128,256]{1,0:T(8,128)S(1)} %get-tuple-element.4), kind=kLoop, calls=%fused_computation | loop fusion | flops 65536 | bytes 524288 | tf_op jit(solution)/shard_map/mul | solution.py:469
